TPU v7x, 32 devices: a whole 2x2x4 slice. The times are simulated.
32 devices in a mesh: pts: 8 (over y, x, core), wlk: 4 (over z).
Axes of the slice: x: 2, y: 2, z: 4, core: 2. Of those that a mesh axis runs over, the one named last changes fastest.
Arguments:
- green_half: bfloat16 [8, 400, 2400], P('wlk'), may hold values from -6 to 6
- collocation: bfloat16 [2400, 9600], P('wlk', 'pts'), may hold values from -0.125 to 0.125
- occupied: bfloat16 [9600, 400], P('pts'), may hold values from -0.0029296875 to 0.0029296875
- kernel: bfloat16 [9600, 9600], P('pts'), may hold values from 0 to 16, as said below
Outputs:
- potential: float32 [8, 9600], P('wlk', 'pts')
- coulomb_energy: float32 [8], P('wlk')
- exchange_energy: float32 [8], P('wlk')
Inputs may be any that keep to these rules, and one draw needn't show every extreme that they name: kernel is symmetric and positive definite: kernel[p, q] equals kernel[q, p].
All inputs are finite; a program needn't handle non-finite values.
Results may differ from a plain program's by a relative error of at most 0.008.
Values may be sent and summed in bfloat16 or wider, within the bound.
A program may use at most 192 MiB of HBM per device.

v0:
```python
import functools

import jax
import jax.numpy as jnp
from jax import lax
from jax.experimental import pallas as pl
from jax.experimental.pallas import tpu as pltpu
from jax.sharding import PartitionSpec as P

TILE = 256


def exchange_kernel(walkers, limit, near_ref, occ_near_ref, far_ref, occ_far_ref, k_ref, out_ref):
    step = pl.program_id(0)

    @pl.when(step == 0)
    def _():
        out_ref[...] = jnp.zeros_like(out_ref)

    rows = occ_near_ref.shape[0]
    kern = k_ref[...].astype(jnp.float32)
    lane = step * TILE + lax.broadcasted_iota(jnp.int32, (8, TILE), 1)
    for w in range(walkers):
        near = jnp.dot(near_ref[w], occ_far_ref[...], preferred_element_type=jnp.float32)
        far = jnp.dot(occ_near_ref[...], far_ref[w], preferred_element_type=jnp.float32)
        term = jnp.sum((kern * near * far).reshape(rows // 8, 8, TILE), axis=0)
        out_ref[w] += jnp.where(lane < limit, term, 0.0)


def exchange_block(low, theta, occupied, far, occ_far, k_block):
    walkers, rows, elec = theta.shape
    points = far.shape[2]
    skip = low // TILE
    out = pl.pallas_call(
        functools.partial(exchange_kernel, walkers, points),
        out_shape=jax.ShapeDtypeStruct((walkers, 8, TILE), jnp.float32),
        grid=(pl.cdiv(points, TILE),),
        in_specs=[
            pl.BlockSpec((walkers, rows, elec), lambda j: (0, 0, 0)),
            pl.BlockSpec((rows, elec), lambda j: (0, 0)),
            pl.BlockSpec((walkers, elec, TILE), lambda j: (0, 0, j)),
            pl.BlockSpec((elec, TILE), lambda j: (0, skip + j)),
            pl.BlockSpec((rows, TILE), lambda j: (0, skip + j)),
        ],
        out_specs=pl.BlockSpec((walkers, 8, TILE), lambda j: (0, 0, 0)),
        compiler_params=pltpu.CompilerParams(vmem_limit_bytes=60 * 1024 * 1024),
        cost_estimate=pl.CostEstimate(
            flops=2 * walkers * 2 * rows * points * elec * 2,
            bytes_accessed=2 * rows * points,
            transcendentals=0,
        ),
        name="exchange",
    )(theta, occupied, far, occ_far, k_block)
    return jnp.sum(out, axis=(1, 2))


def shifted(block, distance):
    devices = lax.axis_size("pts")
    return lax.ppermute(block, "pts", [((i - distance) % devices, i) for i in range(devices)])


def local(green_half, collocation, occupied, kernel):
    rows, elec = occupied.shape
    devices = lax.axis_size("pts")
    position = lax.axis_index("pts")
    cut = pl.cdiv(pl.cdiv(rows, TILE), 2) * TILE
    spans = ((0, cut), (cut, rows))
    far_counts = range(1, devices // 2 + 1)

    occ_turned = occupied.T
    occ_far = {}
    travel = occ_turned
    for stride in far_counts:
        travel = shifted(travel, 1)
        occ_far[stride] = travel
    k_blocks = [
        lax.dynamic_slice_in_dim(kernel, ((position - stride) % devices) * rows, rows, 1)
        for stride in range(devices // 2 + 1)
    ]

    parts = []
    for low, high in spans:
        gathered = lax.all_gather(collocation[:, low:high], "wlk", axis=0, tiled=True)
        if low == 0:
            gathered, *k_blocks = lax.optimization_barrier((gathered, *k_blocks))
        parts.append(
            jnp.einsum("wim,mp->wip", green_half, gathered, preferred_element_type=jnp.float32).astype(
                jnp.bfloat16
            )
        )
    theta_turned = jnp.concatenate(parts, axis=2)
    theta = theta_turned.transpose(0, 2, 1)

    far_parts = [{}, {}]
    for h in range(2):
        travel = parts[h]
        for stride in far_counts:
            travel = shifted(travel, 1)
            far_parts[h][stride] = travel

    density = jnp.sum(
        theta_turned.astype(jnp.float32) * occ_turned.astype(jnp.float32)[None], axis=1
    )
    density_b = density.astype(jnp.bfloat16)
    density_all = lax.all_gather(density_b, "pts", axis=1, tiled=True)
    potential = jnp.einsum("wq,aq->wa", density_all, kernel, preferred_element_type=jnp.float32)

    exchange_sum = exchange_block(0, theta, occupied, theta_turned, occ_turned, k_blocks[0])
    for h, (low, high) in enumerate(spans):
        for stride in far_counts:
            weight = 1.0 if 2 * stride == devices else 2.0
            exchange_sum = exchange_sum + weight * exchange_block(
                low, theta, occupied, far_parts[h][stride], occ_far[stride], k_blocks[stride]
            )
    coulomb = 0.5 * jnp.sum(density * potential, axis=1)
    coulomb_energy, exchange_energy = lax.psum((coulomb, -0.5 * exchange_sum), "pts")
    return (potential, coulomb_energy, exchange_energy)


def solution(mesh):
    placed = (P("wlk", None, None), P("wlk", "pts"), P("pts", None), P("pts", None))
    return jax.shard_map(
        local,
        mesh=mesh,
        in_specs=placed,
        out_specs=(P("wlk", "pts"), P("wlk"), P("wlk")),
        check_vma=False,
    )
```

profile of v0, /device:TPU:0, one launch (start us, length us, event | category | flops | bytes accessed | tf_op | source)
XLA Modules:
  0.0 269.2 jit_solution(4091084247043636954)
XLA Ops:
  11.2 48.8 %all-gather.7.cloned.1.call-done = bf16[4,600,432]{1,2,0:T(8,128)(2,1)} async-done(((bf16[1,600,432]{1,2,0:T(8,128)(2,1)}), bf16[4,600,432]{1,2,0:T(8,128)(2,1)}) %all-gather.7.cloned.1.call-update) | async-done | bytes 2073616 | tf_op jit(solution)/shard_map/all_gather | solution.py:83
  60.0 2.5 copy.63
  62.5 2.7 %reshape.12 = bf16[2400,432,1]{0,1,2:T(8,128)(2,1)} reshape(bf16[4,600,432]{1,0,2:T(4,128)(2,1)S(1)} %copy.63) | data formatting | bytes 4147200
  65.2 5.4 %convolution_convert_fusion = bf16[2,400,432]{2,1,0:T(8,128)(2,1)S(1)} fusion(bf16[2,400,2400]{2,1,0:T(8,128)(2,1)} %param.4, bf16[2400,432,1]{0,1,2:T(8,128)(2,1)} %reshape.12), kind=kOutput, calls=%fused_computation.5 | convolution fusion | flops 1659225600 | bytes 6604800 | tf_op jit(solution)/shard_map/wim,mp->wip/dot_general | solution.py:87
  72.2 11.2 %collective-permute-done.8.far_ref = bf16[2,400,432]{2,1,0:T(8,128)(2,1)S(1)} collective-permute-done((bf16[2,400,432]{2,1,0:T(8,128)(2,1)S(1)}, bf16[2,400,432]{2,1,0:T(8,128)(2,1)S(1)}, u32[]{:S(2)}, u32[]{:S(2)}) %collective-permute-start.8) | collective-permute-done | bytes 691232 | tf_op jit(solution)/shard_map/ppermute | solution.py:59
  83.4 11.1 %collective-permute-done.3.occ_far_ref = bf16[400,1200]{1,0:T(8,128)(2,1)} collective-permute-done((bf16[400,1200]{1,0:T(8,128)(2,1)}, bf16[400,1200]{1,0:T(8,128)(2,1)}, u32[]{:S(2)}, u32[]{:S(2)}) %collective-permute-start.3) | collective-permute-done | bytes 960032 | tf_op jit(solution)/shard_map/ppermute | solution.py:59
  94.5 8.8 %collective-permute-done.9.far_ref = bf16[2,400,432]{2,1,0:T(8,128)(2,1)} collective-permute-done((bf16[2,400,432]{2,1,0:T(8,128)(2,1)S(1)}, bf16[2,400,432]{2,1,0:T(8,128)(2,1)}, u32[]{:S(2)}, u32[]{:S(2)}) %collective-permute-start.9) | collective-permute-done | bytes 691232 | tf_op jit(solution)/shard_map/ppermute | solution.py:59
  103.2 15.3 %constant_dynamic-slice_fusion = (bf16[1200,1200]{1,0:T(8,128)(2,1)}, bf16[1200,1200]{1,0:T(8,128)(2,1)}, bf16[1200,1200]{1,0:T(8,128)(2,1)}, bf16[1200,1200]{1,0:T(8,128)(2,1)}, bf16[1200,1200]{1,0:T(8,128)(2,1)}) fusion(bf16[1200,9600]{1,0:T(8,128)(2,1)} %param.7, s32[]{:T(128)S(6)} %select_n.47, s32[]{:T(128)S(6)} %select_n.45, s32[]{:T(128)S(6)} %select_n.43, ...), kind=kLoop, calls=%fused_computation.8 | loop fusion | bytes 28800020 | tf_op jit(solution)/shard_map/dynamic_slice | solution.py:77
  124.4 8.3 %all-gather.5.cloned.1.call-done = bf16[2400,768]{1,0:T(8,128)(2,1)} async-done(((bf16[600,768]{1,0:T(8,128)(2,1)}), bf16[2400,768]{1,0:T(8,128)(2,1)}) %all-gather.5.cloned.1.call-update) | async-done | bytes 3686416 | tf_op jit(solution)/shard_map/all_gather | solution.py:83
  132.8 7.6 %fusion.2 = bf16[768,2,400]{0,2,1:T(8,128)(2,1)} fusion(bf16[2,400,2400]{2,1,0:T(8,128)(2,1)} %param.4, bf16[2400,768]{1,0:T(8,128)(2,1)} %all-gather.5.cloned.1.call-done), kind=kOutput, calls=%fused_computation.4 | convolution fusion | flops 2949734400 | bytes 8755200 | tf_op jit(solution)/shard_map/wim,mp->wip/dot_general | solution.py:87
  142.1 2.7 pad_maximum_fusion
  144.8 4.3 %copy.68.far_ref = bf16[2,400,1200]{2,1,0:T(8,128)(2,1)} copy(bf16[2,400,1200]{1,2,0:T(8,128)(2,1)} %get-tuple-element.22) | data formatting | bytes 3840000 | tf_op jit(solution)/shard_map/concatenate | solution.py:91
  149.1 6.1 %exchange.14 = f32[2,8,256]{2,1,0:T(8,128)} custom-call(bf16[2,1200,400]{2,1,0:T(8,128)(2,1)} %get-tuple-element.23.near_ref, bf16[1200,400]{1,0:T(8,128)(2,1)} %copy.67.occ_near_ref, bf16[2,400,432]{2,1,0:T(8,128)(2,1)} %copy-done.7, bf16[400,1200]{1,0:T(8,128)(2,1)} %collective-permute-done.1.occ_far_ref, bf16[1200,1200]{1,0:T(8,128)(2,1)} %get-tuple-element.11.k_ref), custom_call_target="tpu_custom_call" | custom-call | flops 3317760000 | bytes 1036800 | tf_op jit(solution)/shard_map/exchange/pallas_call | solution.py:34
  155.2 10.5 %exchange.9 = f32[2,8,256]{2,1,0:T(8,128)} custom-call(bf16[2,1200,400]{2,1,0:T(8,128)(2,1)} %get-tuple-element.23.near_ref, bf16[1200,400]{1,0:T(8,128)(2,1)} %copy.67.occ_near_ref, bf16[2,400,1200]{2,1,0:T(8,128)(2,1)} %copy.68.far_ref, bf16[400,1200]{1,0:T(8,128)(2,1)} %bitcast.27, bf16[1200,1200]{1,0:T(8,128)(2,1)} %get-tuple-element.10.k_ref), custom_call_target="tpu_custom_call" | custom-call | flops 9216000000 | bytes 2880000 | tf_op jit(solution)/shard_map/exchange/pallas_call | solution.py:34
  167.3 6.1 %exchange.15 = f32[2,8,256]{2,1,0:T(8,128)} custom-call(bf16[2,1200,400]{2,1,0:T(8,128)(2,1)} %get-tuple-element.23.near_ref, bf16[1200,400]{1,0:T(8,128)(2,1)} %copy.67.occ_near_ref, bf16[2,400,432]{2,1,0:T(8,128)(2,1)} %collective-permute-done.9.far_ref, bf16[400,1200]{1,0:T(8,128)(2,1)} %collective-permute-done.3.occ_far_ref, ...), custom_call_target="tpu_custom_call" | custom-call | flops 3317760000 | bytes 1036800 | tf_op jit(solution)/shard_map/exchange/pallas_call | solution.py:34
  174.4 6.1 %exchange.16 = f32[2,8,256]{2,1,0:T(8,128)} custom-call(bf16[2,1200,400]{2,1,0:T(8,128)(2,1)} %get-tuple-element.23.near_ref, bf16[1200,400]{1,0:T(8,128)(2,1)} %copy.67.occ_near_ref, bf16[2,400,432]{2,1,0:T(8,128)(2,1)} %collective-permute-done.10.far_ref, bf16[400,1200]{1,0:T(8,128)(2,1)} %collective-permute-done.5.occ_far_ref, ...), custom_call_target="tpu_custom_call" | custom-call | flops 3317760000 | bytes 1036800 | tf_op jit(solution)/shard_map/exchange/pallas_call | solution.py:34
  183.6 9.1 %all-gather.1 = bf16[8,1200,2]{1,2,0:T(2,128)(2,1)S(1)} all-gather(bf16[1,1200,2]{1,2,0:T(2,128)(2,1)S(1)} %convert_bitcast_fusion), channel_id=1, replica_groups=mesh['pts'=8,'wlk'=4] {'pts'}, dimensions={0}, use_global_device_ids=true | all-gather | bytes 43200 | tf_op jit(solution)/shard_map/all_gather | solution.py:105
  193.6 11.4 %multiply_reduce_fusion.1 = (f32[2]{0:T(128)S(1)}, f32[2,1200]{1,0:T(2,128)}) fusion(f32[2,1200]{1,0:T(2,128)S(1)} %multiply_reduce_fusion, bf16[9600,2]{0,1:T(2,128)(2,1)S(1)} %reshape.10, bf16[1200,9600]{1,0:T(8,128)(2,1)} %param.7), kind=kOutput, calls=%fused_computation.6 | convolution fusion | flops 46084800 | bytes 23097608 | tf_op jit(solution)/shard_map/wq,aq->wa/dot_general | solution.py:106
  205.9 6.1 %exchange.17 = f32[2,8,256]{2,1,0:T(8,128)} custom-call(bf16[2,1200,400]{2,1,0:T(8,128)(2,1)} %get-tuple-element.23.near_ref, bf16[1200,400]{1,0:T(8,128)(2,1)} %copy.67.occ_near_ref, bf16[2,400,432]{2,1,0:T(8,128)(2,1)} %copy-done.8, bf16[400,1200]{1,0:T(8,128)(2,1)} %collective-permute-done.7.occ_far_ref, bf16[1200,1200]{1,0:T(8,128)(2,1)} %get-tuple-element.14.k_ref), custom_call_target="tpu_custom_call" | custom-call | flops 3317760000 | bytes 1036800 | tf_op jit(solution)/shard_map/exchange/pallas_call | solution.py:34
  213.1 7.6 %exchange.10 = f32[2,8,256]{2,1,0:T(8,128)} custom-call(bf16[2,1200,400]{2,1,0:T(8,128)(2,1)} %get-tuple-element.23.near_ref, bf16[1200,400]{1,0:T(8,128)(2,1)} %copy.67.occ_near_ref, bf16[2,400,768]{2,1,0:T(8,128)(2,1)} %collective-permute-done.far_ref, bf16[400,1200]{1,0:T(8,128)(2,1)} %collective-permute-done.1.occ_far_ref, ...), custom_call_target="tpu_custom_call" | custom-call | flops 5898240000 | bytes 1843200 | tf_op jit(solution)/shard_map/exchange/pallas_call | solution.py:34
  221.6 7.6 %exchange.11 = f32[2,8,256]{2,1,0:T(8,128)} custom-call(bf16[2,1200,400]{2,1,0:T(8,128)(2,1)} %get-tuple-element.23.near_ref, bf16[1200,400]{1,0:T(8,128)(2,1)} %copy.67.occ_near_ref, bf16[2,400,768]{2,1,0:T(8,128)(2,1)} %collective-permute-done.2.far_ref, bf16[400,1200]{1,0:T(8,128)(2,1)} %collective-permute-done.3.occ_far_ref, ...), custom_call_target="tpu_custom_call" | custom-call | flops 5898240000 | bytes 1843200 | tf_op jit(solution)/shard_map/exchange/pallas_call | solution.py:34
  229.9 7.6 %exchange.12 = f32[2,8,256]{2,1,0:T(8,128)} custom-call(bf16[2,1200,400]{2,1,0:T(8,128)(2,1)} %get-tuple-element.23.near_ref, bf16[1200,400]{1,0:T(8,128)(2,1)} %copy.67.occ_near_ref, bf16[2,400,768]{2,1,0:T(8,128)(2,1)} %copy-done.5, bf16[400,1200]{1,0:T(8,128)(2,1)} %collective-permute-done.5.occ_far_ref, bf16[1200,1200]{1,0:T(8,128)(2,1)} %get-tuple-element.13.k_ref), custom_call_target="tpu_custom_call" | custom-call | flops 5898240000 | bytes 1843200 | tf_op jit(solution)/shard_map/exchange/pallas_call | solution.py:34
  239.4 7.6 %exchange.13 = f32[2,8,256]{2,1,0:T(8,128)} custom-call(bf16[2,1200,400]{2,1,0:T(8,128)(2,1)} %get-tuple-element.23.near_ref, bf16[1200,400]{1,0:T(8,128)(2,1)} %copy.67.occ_near_ref, bf16[2,400,768]{2,1,0:T(8,128)(2,1)} %copy-done.6, bf16[400,1200]{1,0:T(8,128)(2,1)} %collective-permute-done.7.occ_far_ref, bf16[1200,1200]{1,0:T(8,128)(2,1)} %get-tuple-element.14.k_ref), custom_call_target="tpu_custom_call" | custom-call | flops 5898240000 | bytes 1843200 | tf_op jit(solution)/shard_map/exchange/pallas_call | solution.py:34
  247.8 14.6 %all-reduce = (f32[2]{0:T(128)}, f32[2]{0:T(128)}) all-reduce(f32[2]{0:T(128)S(1)} %get-tuple-element.27, f32[2]{0:T(128)S(1)} %get-tuple-element.26), channel_id=1, replica_groups=mesh['pts'=8,'wlk'=4] {'pts'}, use_global_device_ids=true, to_apply=%region_2.3 | all-reduce | flops 4 | bytes 32 | tf_op jit(solution)/shard_map/psum | solution.py:116
  (65 shorter events, 26.2 us)
Async XLA Ops:
  7.2 2.5 copy-start.1
  7.2 3.5 %copy-start = (bf16[1200,400]{0,1:T(8,128)(2,1)S(1)}, bf16[1200,400]{0,1:T(8,128)(2,1)}, u32[]{:S(2)}) copy-start(bf16[1200,400]{0,1:T(8,128)(2,1)} %param.6) | copy-start | bytes 2880004
  7.2 52.8 %all-gather.7.cloned.1.call-start = ((), (), s32[]{:S(2)}) async-start(), calls=%async_computation.1 | async-start | bytes 2764800 | tf_op jit(solution)/shard_map/all_gather | solution.py:83
  9.6 123.2 %all-gather.5.cloned.1.call-start = ((), (), s32[]{:S(2)}) async-start(), calls=%async_computation | async-start | bytes 4608000 | tf_op jit(solution)/shard_map/all_gather | solution.py:83
  10.7 60.1 %collective-permute-start.1 = (bf16[400,1200]{1,0:T(8,128)(2,1)S(1)}, bf16[400,1200]{1,0:T(8,128)(2,1)}, u32[]{:S(2)}, u32[]{:S(2)}) collective-permute-start(bf16[400,1200]{1,0:T(8,128)(2,1)S(1)} %bitcast.28), channel_id=1, source_target_pairs={{28,0},{0,4},{4,8},{8,12},{12,16},{16,20},{20,24},{24,28},{29,1},{... | collective-permute-start | bytes 2880008 | tf_op jit(solution)/shard_map/ppermute | solution.py:59
  70.7 0.9 copy-start.2
  70.7 12.7 %collective-permute-start.8 = (bf16[2,400,432]{2,1,0:T(8,128)(2,1)S(1)}, bf16[2,400,432]{2,1,0:T(8,128)(2,1)S(1)}, u32[]{:S(2)}, u32[]{:S(2)}) collective-permute-start(bf16[2,400,432]{2,1,0:T(8,128)(2,1)S(1)} %convolution_convert_fusion), channel_id=1, source_target_pairs={{28,0},{0,4},{4,8},{8,12},{12,16},{16,20},{20,24},{24,28},{29,1},{... | collective-permute-start | bytes 2073608 | tf_op jit(solution)/shard_map/ppermute | solution.py:59
  71.6 22.9 %collective-permute-start.3 = (bf16[400,1200]{1,0:T(8,128)(2,1)}, bf16[400,1200]{1,0:T(8,128)(2,1)}, u32[]{:S(2)}, u32[]{:S(2)}) collective-permute-start(bf16[400,1200]{1,0:T(8,128)(2,1)} %collective-permute-done.1.occ_far_ref), channel_id=1, source_target_pairs={{28,0},{0,4},{4,8},{8,12},{12,16},{16,20},{20,24},{24,28},{29,1},{... | collective-permute-start | bytes 2880008 | tf_op jit(solution)/shard_map/ppermute | solution.py:59
  83.4 35.1 %copy-start.7 = (bf16[2,400,432]{2,1,0:T(8,128)(2,1)}, bf16[2,400,432]{2,1,0:T(8,128)(2,1)S(1)}, u32[]{:S(2)}) copy-start(bf16[2,400,432]{2,1,0:T(8,128)(2,1)S(1)} %collective-permute-done.8.far_ref) | copy-start | bytes 2073604
  83.4 19.9 %collective-permute-start.9 = (bf16[2,400,432]{2,1,0:T(8,128)(2,1)S(1)}, bf16[2,400,432]{2,1,0:T(8,128)(2,1)}, u32[]{:S(2)}, u32[]{:S(2)}) collective-permute-start(bf16[2,400,432]{2,1,0:T(8,128)(2,1)S(1)} %collective-permute-done.8.far_ref), channel_id=1, source_target_pairs={{28,0},{0,4},{4,8},{8,12},{12,16},{16,20},{20,24},{24,28},{29,1},{... | collective-permute-start | bytes 2073608 | tf_op jit(solution)/shard_map/ppermute | solution.py:59
  94.5 27.8 %collective-permute-start.5 = (bf16[400,1200]{1,0:T(8,128)(2,1)}, bf16[400,1200]{1,0:T(8,128)(2,1)}, u32[]{:S(2)}, u32[]{:S(2)}) collective-permute-start(bf16[400,1200]{1,0:T(8,128)(2,1)} %collective-permute-done.3.occ_far_ref), channel_id=1, source_target_pairs={{28,0},{0,4},{4,8},{8,12},{12,16},{16,20},{20,24},{24,28},{29,1},{... | collective-permute-start | bytes 2880008 | tf_op jit(solution)/shard_map/ppermute | solution.py:59
  103.2 20.9 %collective-permute-start.10 = (bf16[2,400,432]{2,1,0:T(8,128)(2,1)}, bf16[2,400,432]{2,1,0:T(8,128)(2,1)}, u32[]{:S(2)}, u32[]{:S(2)}) collective-permute-start(bf16[2,400,432]{2,1,0:T(8,128)(2,1)} %collective-permute-done.9.far_ref), channel_id=1, source_target_pairs={{28,0},{0,4},{4,8},{8,12},{12,16},{16,20},{20,24},{24,28},{29,1},{... | collective-permute-start | bytes 2073608 | tf_op jit(solution)/shard_map/ppermute | solution.py:59
  122.3 82.7 %collective-permute-start.7 = (bf16[400,1200]{1,0:T(8,128)(2,1)}, bf16[400,1200]{1,0:T(8,128)(2,1)}, u32[]{:S(2)}, u32[]{:S(2)}) collective-permute-start(bf16[400,1200]{1,0:T(8,128)(2,1)} %collective-permute-done.5.occ_far_ref), channel_id=1, source_target_pairs={{28,0},{0,4},{4,8},{8,12},{12,16},{16,20},{20,24},{24,28},{29,1},{... | collective-permute-start | bytes 2880008 | tf_op jit(solution)/shard_map/ppermute | solution.py:59
  124.2 80.8 %collective-permute-start.11 = (bf16[2,400,432]{2,1,0:T(8,128)(2,1)}, bf16[2,400,432]{2,1,0:T(8,128)(2,1)S(1)}, u32[]{:S(2)}, u32[]{:S(2)}) collective-permute-start(bf16[2,400,432]{2,1,0:T(8,128)(2,1)} %collective-permute-done.10.far_ref), channel_id=1, source_target_pairs={{28,0},{0,4},{4,8},{8,12},{12,16},{16,20},{20,24},{24,28},{29,1},{... | collective-permute-start | bytes 2073608 | tf_op jit(solution)/shard_map/ppermute | solution.py:59
  142.0 23.6 %collective-permute-start = (bf16[2,400,768]{2,1,0:T(8,128)(2,1)}, bf16[2,400,768]{2,1,0:T(8,128)(2,1)}, u32[]{:S(2)}, u32[]{:S(2)}) collective-permute-start(bf16[2,400,768]{2,1,0:T(8,128)(2,1)} %bitcast.30), channel_id=1, source_target_pairs={{28,0},{0,4},{4,8},{8,12},{12,16},{16,20},{20,24},{24,28},{29,1},{... | collective-permute-start | bytes 3686408 | tf_op jit(solution)/shard_map/ppermute | solution.py:59
  165.7 7.7 %copy-start.4 = (f32[2,8,256]{2,1,0:T(8,128)S(1)}, f32[2,8,256]{2,1,0:T(8,128)}, u32[]{:S(2)}) copy-start(f32[2,8,256]{2,1,0:T(8,128)} %exchange.9) | copy-start | bytes 49156
  165.7 7.8 %copy-start.3 = (f32[2,8,256]{2,1,0:T(8,128)S(1)}, f32[2,8,256]{2,1,0:T(8,128)}, u32[]{:S(2)}) copy-start(f32[2,8,256]{2,1,0:T(8,128)} %exchange.14) | copy-start | bytes 49156
  165.7 27.3 %collective-permute-start.2 = (bf16[2,400,768]{2,1,0:T(8,128)(2,1)}, bf16[2,400,768]{2,1,0:T(8,128)(2,1)}, u32[]{:S(2)}, u32[]{:S(2)}) collective-permute-start(bf16[2,400,768]{2,1,0:T(8,128)(2,1)} %collective-permute-done.far_ref), channel_id=1, source_target_pairs={{28,0},{0,4},{4,8},{8,12},{12,16},{16,20},{20,24},{24,28},{29,1},{... | collective-permute-start | bytes 3686408 | tf_op jit(solution)/shard_map/ppermute | solution.py:59
  192.9 19.8 %collective-permute-start.4 = (bf16[2,400,768]{2,1,0:T(8,128)(2,1)}, bf16[2,400,768]{2,1,0:T(8,128)(2,1)S(1)}, u32[]{:S(2)}, u32[]{:S(2)}) collective-permute-start(bf16[2,400,768]{2,1,0:T(8,128)(2,1)} %collective-permute-done.2.far_ref), channel_id=1, source_target_pairs={{28,0},{0,4},{4,8},{8,12},{12,16},{16,20},{20,24},{24,28},{29,1},{... | collective-permute-start | bytes 3686408 | tf_op jit(solution)/shard_map/ppermute | solution.py:59
  205.0 0.9 copy-start.8
  212.7 8.0 %copy-start.5 = (bf16[2,400,768]{2,1,0:T(8,128)(2,1)}, bf16[2,400,768]{2,1,0:T(8,128)(2,1)S(1)}, u32[]{:S(2)}) copy-start(bf16[2,400,768]{2,1,0:T(8,128)(2,1)S(1)} %collective-permute-done.4.far_ref) | copy-start | bytes 3686404
  212.7 25.6 %collective-permute-start.6 = (bf16[2,400,768]{2,1,0:T(8,128)(2,1)S(1)}, bf16[2,400,768]{2,1,0:T(8,128)(2,1)S(1)}, u32[]{:S(2)}, u32[]{:S(2)}) collective-permute-start(bf16[2,400,768]{2,1,0:T(8,128)(2,1)S(1)} %collective-permute-done.4.far_ref), channel_id=1, source_target_pairs={{28,0},{0,4},{4,8},{8,12},{12,16},{16,20},{20,24},{24,28},{29,1},{... | collective-permute-start | bytes 3686408 | tf_op jit(solution)/shard_map/ppermute | solution.py:59
  238.3 1.0 copy-start.6
Sparse Core Ops, SparseCore 0:
  9.7 50.2 all-gather.6
  61.6 71.1 all-gather.4
where the time goes:
time: 270 us; the launch traced here: 269 us
  waiting for transfers between devices  88.2 us (33%)
  Pallas kernels  65 us (24%)
  local copies, waits for them, and re-layouts  37.7 us (14%)
  matrix products  24.4 us (9%)
  blocking collectives  23.7 us (9%)
  between operations  14.2 us (5%)
  other arithmetic  11.1 us (4%)
  starting transfers between devices  4.76 us (2%)
    pallas_call x9, Pallas kernels, exchange_block(): pl.pallas_call(functools.partial(exchange_kernel, walkers, points), out_s...  65 us
    all_gather x2, waiting for transfers between devices, local(): lax.all_gather(collocation[:, low:high], 'wlk', axis=0, tiled=True)  57.1 us
    ppermute x12, waiting for transfers between devices, shifted(): lax.ppermute(block, 'pts', [((i - distance) % devices, i) for i in range(...  31.1 us
    dynamic_slice x1, local copies, waits for them, and re-layouts, local(): lax.dynamic_slice_in_dim(kernel, (position - stride) % devices * rows, ro...  15.3 us
    psum x1, blocking collectives, local(): lax.psum((coulomb, -0.5 * exchange_sum), 'pts')  14.6 us
    dot_general x2, matrix products, local(): jnp.einsum('wim,mp->wip', green_half, gathered, preferred_element_type=jn...  13 us
    dot_general x1, matrix products, local(): jnp.einsum('wq,aq->wa', density_all, kernel, preferred_element_type=jnp.f...  11.4 us
    all_gather x1, blocking collectives, local(): density_all = lax.all_gather(density_b, 'pts', axis=1, tiled=True)  9.12 us
  transfers between devices with their start and end apart: 14, of which 5 were waited for; matrix products, arithmetic and copies ran while one was open for 25% of the time, Pallas kernels for 21%

commit v1 on v0

v1 whole, which is shorter than its diff:
```python
import functools

import jax
import jax.numpy as jnp
from jax import lax
from jax.experimental import pallas as pl
from jax.experimental.pallas import tpu as pltpu
from jax.sharding import PartitionSpec as P

CHUNK = 256
LANES = 128
MESH = pl.DeviceIdType.MESH
F32 = jnp.float32
BF16 = jnp.bfloat16


def body(
    bits_n, planes, chunks, frame, piece,
    green_ref, coll_ref, occ_ref, kern_ref,
    pot_ref, coul_ref, exch_ref,
    occ, gin, gs, xg, tht, thr, pht, thq, kal, kst, dens, dq, acc, pot, eall,
    load_sem, kload_sem, zsend, zrecv, psend, precv, tsend, trecv, dsend, drecv, esend, erecv,
):
    n = 1 << bits_n
    rows, elec = occ.shape
    walkers = tht.shape[0]
    orb = coll_ref.shape[0]
    steps = len(chunks)
    me = lax.axis_index("pts")
    z = lax.axis_index("wlk")
    bit = [(me // (1 << t)) % 2 for t in range(bits_n)]

    def peer(d):
        out = me
        for t in range(bits_n):
            if (d >> t) & 1:
                out = out + (1 << t) * (1 - 2 * bit[t])
        return out

    def remote(src, dst, send, recv, to):
        return pltpu.make_async_remote_copy(
            src_ref=src, dst_ref=dst, send_sem=send, recv_sem=recv, device_id=to, device_id_type=MESH
        )

    occ_load = pltpu.make_async_copy(occ_ref, occ, load_sem.at[0])
    occ_load.start()
    x_load = pltpu.make_async_copy(coll_ref, xg.at[z], load_sem.at[1])
    x_load.start()
    g_load = pltpu.make_async_copy(green_ref.at[0], gin, load_sem.at[2])
    g_load.start()

    pieces = []
    total = kern_ref.shape[1]
    for b in range(n):
        start = (rows * b) // LANES * LANES
        width = min(frame + LANES, total - start)
        for r in range(0, rows, piece):
            pieces.append((b, r, start, width, rows * b - start))

    def window(i):
        b, r, start, width, _ = pieces[i]
        return pltpu.make_async_copy(
            kern_ref.at[pl.ds(r, piece), pl.ds(start, width)],
            kst.at[i % 2, :, pl.ds(0, width)],
            kload_sem.at[i % 2],
        )

    window(0).start()
    window(1).start()

    def realign(i):
        b, r, _, width, shift = pieces[i]
        window(i).wait()
        have = min(frame, width - shift)
        kal[b, pl.ds(r, piece), pl.ds(0, have)] = kst[i % 2, :, shift : shift + have]
        if have < frame:
            kal[b, pl.ds(r, piece), pl.ds(have, frame - have)] = jnp.zeros((piece, frame - have), BF16)
        if i + 2 < len(pieces):
            window(i + 2).start()

    barrier = pltpu.get_barrier_semaphore()
    for d in range(1, n):
        pl.semaphore_signal(barrier, inc=1, device_id=(peer(d), z), device_id_type=MESH)

    @pl.when(z > 0)
    def _():
        pl.semaphore_signal(barrier, inc=1, device_id=(me, z - 1), device_id_type=MESH)

    @pl.when(z < planes - 1)
    def _():
        pl.semaphore_signal(barrier, inc=1, device_id=(me, z + 1), device_id_type=MESH)

    ends = (z == 0).astype(jnp.int32) + (z == planes - 1).astype(jnp.int32)
    pl.semaphore_wait(barrier, n - 1 + 2 - ends)

    def z_copy(way, s, k, own):
        lo, wide, _ = chunks[k]
        there = z + (1 if way else -1)
        src = coll_ref.at[:, pl.ds(lo, wide)] if own else xg.at[s, :, pl.ds(lo, wide)]
        return remote(
            src, xg.at[s, :, pl.ds(lo, wide)], zsend.at[way, s, k], zrecv.at[s, k], (me, there)
        )

    def z_own(k):
        @pl.when(z > 0)
        def _():
            z_copy(0, z, k, True).start()

        @pl.when(z < planes - 1)
        def _():
            z_copy(1, z, k, True).start()

    def z_pass(k, j):
        for way, ok, more, s in (
            (0, z + j < planes, z > 0, z + j),
            (1, z - j >= 0, z < planes - 1, z - j),
        ):
            @pl.when(ok)
            def _():
                z_copy(way, s, k, False).wait_recv()

                @pl.when(more)
                def _():
                    z_copy(way, s, k, False).start()

    def z_done(k):
        for j in range(planes):
            for way, ok, s in (
                (0, (z + j < planes) & (z > 0), z + j),
                (1, (z - j >= 0) & (z < planes - 1), z - j),
            ):
                @pl.when(ok)
                def _():
                    z_copy(way, s, k, j == 0).wait_send()

    def occ_copy(t, d):
        return remote(
            pht.at[d], pht.at[d ^ (1 << t)], psend.at[t, d], precv.at[d ^ (1 << t)], (peer(1 << t), z)
        )

    def th_copy(t, d, k):
        lo, _, wide = chunks[k]
        if d == 0:
            src = tht.at[1 - bit[t], :, pl.ds(lo, wide)]
        else:
            src = thq.at[d, :, pl.ds(lo, wide)]
        e = d ^ (1 << t)
        return remote(
            src, thq.at[e, :, pl.ds(lo, wide)], tsend.at[t, d, k], trecv.at[e, k], (peer(1 << t), z)
        )

    def d_copy(d, k):
        lo, _, wide = chunks[k]
        return remote(
            dq.at[0, :, pl.ds(lo, wide)], dq.at[d, :, pl.ds(lo, wide)],
            dsend.at[d, k], drecv.at[d, k], (peer(d), z),
        )

    z_own(0)
    if steps > 1:
        z_own(1)

    acc[...] = jnp.zeros_like(acc)
    pot[...] = jnp.zeros_like(pot)
    dens[...] = jnp.zeros_like(dens)
    dq[0] = jnp.zeros_like(dq[0])
    if rows < frame:
        for w in range(walkers):
            tht[w, :, pl.ds(rows, frame - rows)] = jnp.zeros((elec, frame - rows), BF16)
        pht[0, :, pl.ds(rows, frame - rows)] = jnp.zeros((elec, frame - rows), BF16)
    occ_load.wait()
    for lo, wide, _ in chunks:
        pht[0, :, pl.ds(lo, wide)] = occ[pl.ds(lo, wide), :].T

    chip_bits = list(range(1, bits_n))
    held = [0]
    sent = []
    plan = []
    for t in chip_bits + [0]:
        plan.append((t, list(held)))
        held = held + [d ^ (1 << t) for d in held]
    for t, _ in plan:
        occ_copy(t, 0).start()

    def occ_pass(step):
        t, deltas = plan[step]
        for d in deltas:
            e = d ^ (1 << t)
            occ_copy(t, d).wait_recv()
            for later, ds in plan[step + 1 :]:
                if e in ds:
                    occ_copy(later, e).start()

    for w in range(walkers):
        g_load.wait()
        for s in range(planes):
            gs[s, pl.ds(w * elec, elec), :] = gin[:, s * orb : (s + 1) * orb]
        if w + 1 < walkers:
            g_load = pltpu.make_async_copy(green_ref.at[w + 1], gin, load_sem.at[2])
            g_load.start()

    at = 0
    share = len(pieces) // 4
    for i in range(share):
        realign(i)
    at = share
    z_first = [1] if planes > 1 else []
    for j in z_first:
        z_pass(0, j)
    for step in range(len(plan) - 1):
        for i in range(at, at + share):
            realign(i)
        at += share
        occ_pass(step)
    for i in range(at, len(pieces)):
        realign(i)
    occ_pass(len(plan) - 1)

    th_plan = []
    held = [0]
    for t in list(reversed(chip_bits)) + [0]:
        th_plan.append((t, list(held)))
        held = held + [d ^ (1 << t) for d in held]

    def theta(k):
        lo, valid, wide = chunks[k]
        total = None
        for s in range(planes):
            part = jnp.dot(gs[s], xg[s, :, pl.ds(lo, valid)], preferred_element_type=F32)
            total = part if total is None else total + part
        for w in range(walkers):
            one = total[w * elec : (w + 1) * elec].astype(BF16)
            tht[w, :, pl.ds(lo, valid)] = one
        for w in range(walkers):
            turned = tht[w, :, pl.ds(lo, valid)]
            thr[w, pl.ds(lo, valid), :] = turned.T
            value = jnp.sum(
                turned.astype(F32) * pht[0, :, pl.ds(lo, valid)].astype(F32), axis=0, keepdims=True
            )
            dens[pl.ds(w, 1), pl.ds(lo, valid)] = value
        dq[0, pl.ds(0, 8), pl.ds(lo, wide)] = dens[pl.ds(0, 8), pl.ds(lo, wide)].astype(BF16)
        for t, _ in th_plan:
            th_copy(t, 0, k).start()
        for d in range(1, n):
            d_copy(d, k).start()

    def th_pass(k):
        for step, (t, deltas) in enumerate(th_plan[:-1]):
            for d in deltas:
                e = d ^ (1 << t)
                th_copy(t, d, k).wait_recv()
                for later, ds in th_plan[step + 1 :]:
                    if e in ds:
                        th_copy(later, e, k).start()

    def th_last(k):
        t, deltas = th_plan[-1]
        for d in deltas:
            th_copy(t, d, k).wait_recv()
        for d in range(1, n):
            d_copy(d, k).wait_recv()

    def fold(w, b, near_lhs, far_lhs, near_rhs, far_rhs, p0, pm, q0, qw, weight):
        near = jnp.dot(near_lhs, near_rhs, preferred_element_type=F32)
        far = jnp.dot(far_lhs, far_rhs, preferred_element_type=F32)
        term = near * far * kal[b, pl.ds(p0, pm), pl.ds(q0, qw)].astype(F32)
        acc[w, :, pl.ds(0, qw)] += weight * jnp.sum(term.reshape(pm // 8, 8, qw), axis=0)

    def exchange(k):
        lo, valid, wide = chunks[k]
        full = lo + valid

        @pl.loop(0, walkers)
        def _(w):
            if lo > 0:
                fold(w, me, thr[w, pl.ds(0, lo), :], occ[pl.ds(0, lo), :], pht[0, :, pl.ds(lo, wide)],
                     tht[w, :, pl.ds(lo, wide)], 0, lo, lo, wide, 2.0)
            fold(w, me, thr[w, pl.ds(lo, valid), :], occ[pl.ds(lo, valid), :], pht[0, :, pl.ds(lo, wide)],
                 tht[w, :, pl.ds(lo, wide)], lo, valid, lo, wide, 1.0)

        th_last(k)

        @pl.loop(1, n)
        def _(d):
            b = jnp.int32(0)
            w = jnp.int32(0)
            for t in range(bits_n):
                b = b + (1 << t) * ((bit[t] + d // (1 << t)) % 2)
                w = w + jnp.where(d // (1 << t) == 1, bit[t], 0)
            fold(w, b, thr[w, pl.ds(0, full), :], occ[pl.ds(0, full), :], pht[d, :, pl.ds(lo, wide)],
                 thq[d, :, pl.ds(lo, wide)], 0, full, lo, wide, 2.0)
            if k > 0:
                @pl.loop(0, k)
                def _(j):
                    q0 = pl.multiple_of(j * CHUNK, CHUNK)
                    fold(w, b, thr[w, pl.ds(lo, valid), :], occ[pl.ds(lo, valid), :],
                         pht[d, :, pl.ds(q0, CHUNK)], thq[d, :, pl.ds(q0, CHUNK)],
                         lo, valid, q0, CHUNK, 2.0)

        @pl.loop(0, n)
        def _(d):
            b = jnp.int32(0)
            for t in range(bits_n):
                b = b + (1 << t) * ((bit[t] + d // (1 << t)) % 2)
            pot[...] += lax.dot_general(
                kal[b, :, pl.ds(lo, wide)], dq[d, :, pl.ds(lo, wide)],
                (((1,), (1,)), ((), ())), preferred_element_type=F32,
            )

    for k in range(steps):
        for j in range(1, planes):
            if not (k == 0 and j in z_first):
                z_pass(k, j)
        if k + 2 < steps:
            z_own(k + 2)
        if k == 0:
            x_load.wait()
        theta(k)
        if k > 0:
            exchange(k - 1)
        th_pass(k)
    exchange(steps - 1)

    pot_rows = pot[...].T
    pot_ref[...] = pot_rows[:walkers, :]
    for w in range(walkers):
        eall[me, pl.ds(w, 1), :] = jnp.full((1, LANES), 0.5 * jnp.sum(dens[pl.ds(w, 1), pl.ds(0, rows)] * pot_rows[w : w + 1, :]), F32)
        eall[me, pl.ds(walkers + w, 1), :] = jnp.full((1, LANES), -0.5 * jnp.sum(acc[w]), F32)

    def e_copy(d):
        return remote(eall.at[me], eall.at[me], esend.at[d], erecv.at[d], (peer(d), z))

    def e_wait(d):
        return remote(eall.at[peer(d)], eall.at[peer(d)], esend.at[d], erecv.at[d], (peer(d), z))

    for d in range(1, n):
        e_copy(d).start()
    for d in range(1, n):
        e_wait(d).wait_recv()
    whole = eall[0]
    for b in range(1, n):
        whole = whole + eall[b]
    for w in range(walkers):
        coul_ref[w] = whole[w, 0]
        exch_ref[w] = whole[walkers + w, 0]

    for d in range(1, n):
        e_copy(d).wait_send()
    for t, deltas in plan:
        for d in deltas:
            occ_copy(t, d).wait_send()
    for k in range(steps):
        z_done(k)
        for t, deltas in th_plan:
            for d in deltas:
                th_copy(t, d, k).wait_send()
        for d in range(1, n):
            d_copy(d, k).wait_send()


def local(green_half, collocation, occupied, kernel):
    walkers, elec, _ = green_half.shape
    orb, rows = collocation.shape
    n = lax.axis_size("pts")
    planes = lax.axis_size("wlk")
    bits_n = n.bit_length() - 1
    frame = pl.cdiv(rows, LANES) * LANES
    chunks = []
    for lo in range(0, rows, CHUNK):
        chunks.append((lo, min(CHUNK, rows - lo), min(CHUNK, frame - lo)))
    steps = len(chunks)
    piece = max([r for r in range(16, 256, 16) if rows % r == 0] or [rows])
    anywhere = pl.BlockSpec(memory_space=pl.ANY)
    smem = pl.BlockSpec(memory_space=pltpu.SMEM)
    dma = pltpu.SemaphoreType.DMA
    potential, coulomb, exchange = pl.pallas_call(
        functools.partial(body, bits_n, planes, tuple(chunks), frame, piece),
        out_shape=(
            jax.ShapeDtypeStruct((walkers, rows), F32),
            jax.ShapeDtypeStruct((walkers,), F32),
            jax.ShapeDtypeStruct((walkers,), F32),
        ),
        in_specs=[anywhere] * 4,
        out_specs=(pl.BlockSpec(memory_space=pltpu.VMEM), smem, smem),
        scratch_shapes=[
            pltpu.VMEM((rows, elec), BF16),
            pltpu.VMEM((elec, green_half.shape[2]), BF16),
            pltpu.VMEM((planes, walkers * elec, orb), BF16),
            pltpu.VMEM((planes, orb, rows), BF16),
            pltpu.VMEM((walkers, elec, frame), BF16),
            pltpu.VMEM((walkers, rows, elec), BF16),
            pltpu.VMEM((n, elec, frame), BF16),
            pltpu.VMEM((n, elec, frame), BF16),
            pltpu.VMEM((n, rows, frame), BF16),
            pltpu.VMEM((2, piece, frame + LANES), BF16),
            pltpu.VMEM((8, frame), F32),
            pltpu.VMEM((n, 16, frame), BF16),
            pltpu.VMEM((walkers, 8, CHUNK), F32),
            pltpu.VMEM((rows, 16), F32),
            pltpu.VMEM((n, 8, LANES), F32),
            dma((3,)),
            dma((2,)),
            dma((2, planes, steps)),
            dma((planes, steps)),
            dma((bits_n, n)),
            dma((n,)),
            dma((bits_n, n, steps)),
            dma((n, steps)),
            dma((n, steps)),
            dma((n, steps)),
            dma((n,)),
            dma((n,)),
        ],
        compiler_params=pltpu.CompilerParams(
            collective_id=0, has_side_effects=True, vmem_limit_bytes=67043328
        ),
        name="energy",
    )(green_half, collocation, occupied, kernel)
    return potential, coulomb, exchange


def solution(mesh):
    placed = (P("wlk", None, None), P("wlk", "pts"), P("pts", None), P("pts", None))
    return jax.shard_map(
        local,
        mesh=mesh,
        in_specs=placed,
        out_specs=(P("wlk", "pts"), P("wlk"), P("wlk")),
        check_vma=False,
    )
```

time: 270 us -> 204 us (0.76)
  Pallas kernels: 65 us -> 197 us
  waiting for transfers between devices: 88.2 us -> 0 us
  local copies, waits for them, and re-layouts: 37.7 us -> 5.95 us
  matrix products: 24.4 us -> 0 us
  blocking collectives: 23.7 us -> 0 us
  between operations: 14.2 us -> 0.64 us
  other arithmetic: 11.1 us -> 0 us
  starting transfers between devices: 4.76 us -> 0 us
    pallas_call x9 -> x1, Pallas kernels: 65 us -> 197 us  [local(): pl.pallas_call(functools.partial(body, bits_n, planes, tuple(chunks), fra...]
    all_gather x2 -> x0, waiting for transfers between devices: 57.1 us -> none  [local(): lax.all_gather(collocation[:, low:high], 'wlk', axis=0, tiled=True)]
    ppermute x12 -> x0, waiting for transfers between devices: 31.1 us -> none  [shifted(): lax.ppermute(block, 'pts', [((i - distance) % devices, i) for i in range(...]
    dot_general x3 -> x0, matrix products: 24.4 us -> none  [the longest x2 13 us: local(): jnp.einsum('wim,mp->wip', green_half, gathered, preferred_element_type=jn...]
    dynamic_slice x1 -> x0, local copies, waits for them, and re-layouts: 15.3 us -> none  [local(): lax.dynamic_slice_in_dim(kernel, (position - stride) % devices * rows, ro...]
    psum x1 -> x0, blocking collectives: 14.6 us -> none  [local(): lax.psum((coulomb, -0.5 * exchange_sum), 'pts')]
    all_gather x1 -> x0, blocking collectives: 9.12 us -> none  [local(): density_all = lax.all_gather(density_b, 'pts', axis=1, tiled=True)]
    reduce_sum x10 -> x0, other arithmetic: 8.29 us -> none  [the longest x9 5.9 us: exchange_block(): return jnp.sum(out, axis=(1, 2))]
  transfers between devices with their start and end apart: 14 -> 0, of which waited for: 5 -> 0; matrix products, arithmetic and copies ran while one was open for 25% -> 0% of each run, Pallas kernels for 21% -> 0%
where the time goes in v1:
time: 204 us; the launch traced here: 203 us
  Pallas kernels  197 us (97%)
  local copies, waits for them, and re-layouts  5.95 us (3%)
    pallas_call x1, Pallas kernels, local(): pl.pallas_call(functools.partial(body, bits_n, planes, tuple(chunks), fra...  197 us
    unnamed x4, local copies, waits for them, and re-layouts  5.95 us

profile of v1, /device:TPU:0, one launch (start us, length us, event | category | flops | bytes accessed | tf_op | source)
XLA Modules:
  0.0 203.4 jit_solution(6649291509161385907)
XLA Ops:
  0.6 2.4 %copy.7.occ_ref = bf16[1200,400]{1,0:T(8,128)(2,1)} copy(bf16[1200,400]{0,1:T(8,128)(2,1)} %param.6) | data formatting | bytes 1920000 | tf_op args[2]
  3.0 196.8 %energy.1 = (f32[2,1200]{1,0:T(2,128)}, f32[2]{0:T(128)}, f32[2]{0:T(128)}) custom-call(bf16[2,400,2400]{2,1,0:T(8,128)(2,1)} %green_ref.1, bf16[600,1200]{1,0:T(8,128)(2,1)} %coll_ref.1, bf16[1200,400]{1,0:T(8,128)(2,1)} %copy.7.occ_ref, bf16[1200,9600]{1,0:T(8,128)(2,1)} %kern_ref.1), custom_call_target="tpu_custom_call" | custom-call | tf_op jit(solution)/shard_map/energy/pallas_call | solution.py:376
  199.8 1.3 copy.11
  201.1 1.2 copy.12
  202.3 1.1 copy.13

commit v2 on v1

v2 whole, which is shorter than its diff:
```python
import functools

import jax
import jax.numpy as jnp
from jax import lax
from jax.experimental import pallas as pl
from jax.experimental.pallas import tpu as pltpu
from jax.sharding import PartitionSpec as P

CHUNK = 256
LANES = 128
MESH = pl.DeviceIdType.MESH
F32 = jnp.float32
BF16 = jnp.bfloat16


def body(
    bits_n, planes, chunks, frame, piece,
    green_ref, coll_ref, occ_ref, kern_ref,
    pot_ref, coul_ref, exch_ref,
    occ, gin, gs, xg, tht, thr, pht, thq, kal, kext, dens, dq, acc, pot, eall,
    load_sem, kload_sem, zsend, zrecv, psend, precv, tsend, trecv, dsend, drecv, esend, erecv,
):
    n = 1 << bits_n
    rows, elec = occ.shape
    walkers = tht.shape[0]
    orb = coll_ref.shape[0]
    steps = len(chunks)
    me = lax.axis_index("pts")
    z = lax.axis_index("wlk")
    bit = [(me // (1 << t)) % 2 for t in range(bits_n)]

    def peer(d):
        out = me
        for t in range(bits_n):
            if (d >> t) & 1:
                out = out + (1 << t) * (1 - 2 * bit[t])
        return out

    def remote(src, dst, send, recv, to):
        return pltpu.make_async_remote_copy(
            src_ref=src, dst_ref=dst, send_sem=send, recv_sem=recv, device_id=to, device_id_type=MESH
        )

    occ_load = pltpu.make_async_copy(occ_ref, pht.at[0], load_sem.at[0])
    occ_load.start()
    x_load = pltpu.make_async_copy(coll_ref, xg.at[z], load_sem.at[1])
    x_load.start()
    g_load = pltpu.make_async_copy(green_ref.at[0], gin, load_sem.at[2])
    g_load.start()

    windows = []
    spill = 0
    for b in range(n):
        start = (rows * b) // LANES * LANES
        shift = rows * b - start
        over = shift + rows > frame
        windows.append((start, min(frame, kern_ref.shape[1] - start), shift, spill if over else None))
        spill += over

    def window(b):
        start, width, _, extra = windows[b]
        copies = [
            pltpu.make_async_copy(
                kern_ref.at[:, pl.ds(start, width)], kal.at[b, :, pl.ds(0, width)], kload_sem.at[0, b]
            )
        ]
        if extra is not None:
            copies.append(
                pltpu.make_async_copy(
                    kern_ref.at[:, pl.ds(start + frame, LANES)], kext.at[extra], kload_sem.at[1, b]
                )
            )
        return copies

    for b in range(n):
        for copy in window(b):
            copy.start()

    def realign(b):
        _, width, shift, extra = windows[b]
        for copy in window(b):
            copy.wait()
        if shift > 0:
            @pl.loop(0, rows // piece)
            def _(i):
                r = pl.multiple_of(i * piece, piece)
                part = kal[b, pl.ds(r, piece), :]
                if extra is not None:
                    part = jnp.concatenate([part, kext[extra, pl.ds(r, piece), :]], axis=1)
                kal[b, pl.ds(r, piece), pl.ds(0, rows)] = part[:, shift : shift + rows]

    barrier = pltpu.get_barrier_semaphore()
    for d in range(1, n):
        pl.semaphore_signal(barrier, inc=1, device_id=(peer(d), z), device_id_type=MESH)

    @pl.when(z > 0)
    def _():
        pl.semaphore_signal(barrier, inc=1, device_id=(me, z - 1), device_id_type=MESH)

    @pl.when(z < planes - 1)
    def _():
        pl.semaphore_signal(barrier, inc=1, device_id=(me, z + 1), device_id_type=MESH)

    ends = (z == 0).astype(jnp.int32) + (z == planes - 1).astype(jnp.int32)
    pl.semaphore_wait(barrier, n - 1 + 2 - ends)

    def z_copy(way, s, k, own):
        lo, wide = chunks[k]
        there = z + (1 if way else -1)
        src = coll_ref.at[:, pl.ds(lo, wide)] if own else xg.at[s, :, pl.ds(lo, wide)]
        return remote(
            src, xg.at[s, :, pl.ds(lo, wide)], zsend.at[way, s, k], zrecv.at[s, k], (me, there)
        )

    def z_own(k):
        @pl.when(z > 0)
        def _():
            z_copy(0, z, k, True).start()

        @pl.when(z < planes - 1)
        def _():
            z_copy(1, z, k, True).start()

    def ways(j):
        return ((0, z + j < planes, z > 0, z + j), (1, z - j >= 0, z < planes - 1, z - j))

    def z_pass(k, j):
        for way, ok, more, s in ways(j):
            @pl.when(ok & more)
            def _():
                z_copy(way, s, k, False).wait_recv()
                z_copy(way, s, k, False).start()

    def z_take(k):
        for j in range(1, planes):
            for way, ok, more, s in ways(j):
                @pl.when(ok & jnp.logical_not(more))
                def _():
                    z_copy(way, s, k, False).wait_recv()

    def z_done(k):
        for j in range(planes):
            for way, ok, s in (
                (0, (z + j < planes) & (z > 0), z + j),
                (1, (z - j >= 0) & (z < planes - 1), z - j),
            ):
                @pl.when(ok)
                def _():
                    z_copy(way, s, k, j == 0).wait_send()

    def occ_copy(t, d):
        return remote(
            pht.at[d], pht.at[d ^ (1 << t)], psend.at[t, d], precv.at[d ^ (1 << t)], (peer(1 << t), z)
        )

    def th_copy(t, d, k):
        lo, wide = chunks[k]
        if d == 0:
            src = tht.at[1 - bit[t], :, pl.ds(lo, wide)]
        else:
            src = thq.at[d - 1, :, pl.ds(lo, wide)]
        e = d ^ (1 << t)
        return remote(
            src, thq.at[e - 1, :, pl.ds(lo, wide)], tsend.at[t, d, k], trecv.at[e, k], (peer(1 << t), z)
        )

    def d_copy(d, k):
        lo, wide = chunks[k]
        return remote(
            dq.at[0, :, pl.ds(lo, wide)], dq.at[d, :, pl.ds(lo, wide)],
            dsend.at[d, k], drecv.at[d, k], (peer(d), z),
        )

    z_own(0)
    if steps > 1:
        z_own(1)

    acc[...] = jnp.zeros_like(acc)
    pot[...] = jnp.zeros_like(pot)
    dens[...] = jnp.zeros_like(dens)
    occ_load.wait()
    for lo, wide in chunks:
        occ[pl.ds(lo, wide), :] = pht[0, :, pl.ds(lo, wide)].T

    chip_bits = list(range(1, bits_n))
    held = [0]
    sent = []
    plan = []
    for t in chip_bits + [0]:
        plan.append((t, list(held)))
        held = held + [d ^ (1 << t) for d in held]
    for t, _ in plan:
        occ_copy(t, 0).start()

    def occ_pass(step):
        t, deltas = plan[step]
        for d in deltas:
            e = d ^ (1 << t)
            occ_copy(t, d).wait_recv()
            for later, ds in plan[step + 1 :]:
                if e in ds:
                    occ_copy(later, e).start()

    for w in range(walkers):
        g_load.wait()
        for s in range(planes):
            gs[s, pl.ds(w * elec, elec), :] = gin[:, s * orb : (s + 1) * orb]
        if w + 1 < walkers:
            g_load = pltpu.make_async_copy(green_ref.at[w + 1], gin, load_sem.at[2])
            g_load.start()

    th_plan = []
    held = [0]
    for t in list(reversed(chip_bits)) + [0]:
        th_plan.append((t, list(held)))
        held = held + [d ^ (1 << t) for d in held]

    def theta(k):
        lo, valid = chunks[k]
        total = None
        for s in range(planes):
            part = jnp.dot(gs[s], xg[s, :, pl.ds(lo, valid)], preferred_element_type=F32)
            total = part if total is None else total + part
        for w in range(walkers):
            one = total[w * elec : (w + 1) * elec].astype(BF16)
            tht[w, :, pl.ds(lo, valid)] = one
        for w in range(walkers):
            turned = tht[w, :, pl.ds(lo, valid)]
            thr[w, pl.ds(lo, valid), :] = turned.T
            value = jnp.sum(
                turned.astype(F32) * pht[0, :, pl.ds(lo, valid)].astype(F32), axis=0, keepdims=True
            )
            dens[pl.ds(w, 1), pl.ds(lo, valid)] = value
        dq[0, :, pl.ds(lo, valid)] = dens[:, pl.ds(lo, valid)].astype(BF16)
        for t, _ in th_plan:
            th_copy(t, 0, k).start()
        for d in range(1, n):
            d_copy(d, k).start()

    arrivals = []
    for t, deltas in th_plan[-1:] + th_plan[:-1]:
        for d in deltas:
            if t > 0 or d == 0:
                arrivals.append((t, d))
    for d in th_plan[-1][1]:
        if d > 0:
            arrivals.append((0, d))
    order = [d ^ (1 << t) for t, d in arrivals]

    arrived = set()

    def arrive(i, k):
        if (i, k) in arrived:
            return
        arrived.add((i, k))
        t, d = arrivals[i]
        e = order[i]
        th_copy(t, d, k).wait_recv()
        for later, ds in th_plan:
            if e in ds:
                th_copy(later, e, k).start()
        d_copy(e, k).wait_recv()

    def lanes_to(x, width):
        out = x[:, :width]
        for at in range(width, x.shape[1], width):
            out = out + x[:, at : at + width]
        return out

    def spread(d, kf, p0, pm, q0, qw):
        for w in range(walkers):
            u = kf * dq[d, pl.ds(w, 1), pl.ds(q0, qw)].astype(F32)
            if qw > LANES and qw % LANES:
                cut = qw // LANES * LANES
                pot[w, pl.ds(p0, pm), :] += lanes_to(u[:, :cut], LANES)
                pot[w, pl.ds(p0, pm), pl.ds(0, qw - cut)] += u[:, cut:]
            else:
                part = lanes_to(u, min(LANES, qw))
                pot[w, pl.ds(p0, pm), pl.ds(0, min(LANES, qw))] += part

    def fold(w, b, d, far_rhs, p0, pm, q0, qw, weight):
        near = jnp.dot(thr[w, pl.ds(p0, pm), :], pht[d, :, pl.ds(q0, qw)], preferred_element_type=F32)
        far = jnp.dot(occ[pl.ds(p0, pm), :], far_rhs, preferred_element_type=F32)
        kf = kal[b, pl.ds(p0, pm), pl.ds(q0, qw)].astype(F32)
        term = near * far * kf
        term = lanes_to(jnp.sum(term.reshape(pm // 8, 8, qw), axis=0), min(qw, CHUNK))
        acc[w, :, pl.ds(0, min(qw, CHUNK))] += weight * term
        return kf

    def pair(d):
        b = jnp.int32(0)
        w = jnp.int32(0)
        for t in range(bits_n):
            b = b + (1 << t) * ((bit[t] + d // (1 << t)) % 2)
            w = w + jnp.where(d // (1 << t) == 1, bit[t], 0)
        return b, w

    def exchange_old(k):
        lo, wide = chunks[k]
        if k == 0:
            return

        @pl.loop(1, n)
        def _(d):
            b, w = pair(d)
            kf = fold(w, b, d, thq[d - 1, :, pl.ds(0, lo)], lo, wide, 0, lo, 2.0)
            spread(d, kf, lo, wide, 0, lo)

    def exchange_own(k):
        lo, wide = chunks[k]

        @pl.loop(0, walkers)
        def _(w):
            rhs = tht[w, :, pl.ds(lo, wide)]
            if lo > 0:
                fold(w, me, 0, rhs, 0, lo, lo, wide, 2.0)
            fold(w, me, 0, rhs, lo, wide, lo, wide, 1.0)

        spread(0, kal[me, :, pl.ds(lo, wide)].astype(F32), 0, rows, lo, wide)

    def exchange_new(k, services):
        lo, wide = chunks[k]
        full = lo + wide

        @pl.loop(0, n - 1)
        def _(i):
            d = jnp.int32(0)
            for j in range(n - 1):
                d = d + jnp.where(i == j, order[j], 0)

                @pl.when(i == j)
                def _():
                    arrive(j, k)
                    for serve in services.get(j, ()):
                        serve()

            b, w = pair(d)
            kf = fold(w, b, d, thq[d - 1, :, pl.ds(lo, wide)], 0, full, lo, wide, 2.0)
            spread(d, kf, 0, full, lo, wide)

    def near_pass(k):
        if k < steps:
            z_pass(k, 1)

    def far_pass(k):
        if k < steps:
            for j in range(2, planes):
                z_pass(k, j)

    def own_send(k):
        if 1 < k < steps:
            z_own(k)

    def first_arrivals(k):
        for i, (t, d) in enumerate(arrivals):
            if t > 0 and d == 0:
                arrive(i, k)

    def exchange_all(k, services):
        exchange_old(k)
        exchange_own(k)
        exchange_new(k, services)

    near_pass(0)
    for b in range(n):
        realign(b)
    near_pass(1)
    own_send(2)
    occ_pass(0)
    far_pass(0)
    z_take(0)
    x_load.wait()
    theta(0)
    far_pass(1)
    near_pass(2)
    own_send(3)
    first_arrivals(0)
    for step in range(1, len(plan)):
        occ_pass(step)
    for k in range(1, steps):
        if k == steps - 1:
            exchange_old(k - 1)
            exchange_own(k - 1)
            first_arrivals(k - 1)
        z_take(k)
        theta(k)
        far_pass(k + 1)
        near_pass(k + 2)
        own_send(k + 3)
        if k == 1 and k < steps - 1:
            exchange_all(0, {n - 2: [functools.partial(first_arrivals, 1)]})
        if k == steps - 1:
            exchange_new(k - 1, {n - 3: [functools.partial(first_arrivals, k)]})
        elif k < steps - 2:
            exchange_all(k, {})
    exchange_old(steps - 1)
    exchange_own(steps - 1)
    exchange_new(steps - 1, {})

    pot_rows = []
    for w in range(walkers):
        pot_rows.append(jnp.sum(pot[w].T, axis=0, keepdims=True))
        pot_ref[pl.ds(w, 1), :] = pot_rows[w]
    for w in range(walkers):
        eall[me, pl.ds(w, 1), :] = jnp.full((1, LANES), 0.5 * jnp.sum(dens[pl.ds(w, 1), :] * pot_rows[w]), F32)
        eall[me, pl.ds(walkers + w, 1), :] = jnp.full((1, LANES), -0.5 * jnp.sum(acc[w]), F32)

    def e_copy(d):
        return remote(eall.at[me], eall.at[me], esend.at[d], erecv.at[d], (peer(d), z))

    def e_wait(d):
        return remote(eall.at[peer(d)], eall.at[peer(d)], esend.at[d], erecv.at[d], (peer(d), z))

    for d in range(1, n):
        e_copy(d).start()
    for d in range(1, n):
        e_wait(d).wait_recv()
    whole = eall[0]
    for b in range(1, n):
        whole = whole + eall[b]
    for w in range(walkers):
        coul_ref[w] = whole[w, 0]
        exch_ref[w] = whole[walkers + w, 0]

    for d in range(1, n):
        e_copy(d).wait_send()
    for t, deltas in plan:
        for d in deltas:
            occ_copy(t, d).wait_send()
    for k in range(steps):
        z_done(k)
        for t, deltas in th_plan:
            for d in deltas:
                th_copy(t, d, k).wait_send()
        for d in range(1, n):
            d_copy(d, k).wait_send()


def local(green_half, collocation, occupied, kernel):
    walkers, elec, _ = green_half.shape
    orb, rows = collocation.shape
    n = lax.axis_size("pts")
    planes = lax.axis_size("wlk")
    bits_n = n.bit_length() - 1
    frame = pl.cdiv(rows, LANES) * LANES
    chunks = []
    for lo in range(0, rows, CHUNK):
        chunks.append((lo, min(CHUNK, rows - lo)))
    steps = len(chunks)
    spills = max(1, sum((rows * b) % LANES + rows > frame for b in range(n)))
    piece = max([r for r in range(16, 256, 16) if rows % r == 0] or [rows])
    anywhere = pl.BlockSpec(memory_space=pl.ANY)
    smem = pl.BlockSpec(memory_space=pltpu.SMEM)
    dma = pltpu.SemaphoreType.DMA
    potential, coulomb, exchange = pl.pallas_call(
        functools.partial(body, bits_n, planes, tuple(chunks), frame, piece),
        out_shape=(
            jax.ShapeDtypeStruct((walkers, rows), F32),
            jax.ShapeDtypeStruct((walkers,), F32),
            jax.ShapeDtypeStruct((walkers,), F32),
        ),
        in_specs=[anywhere] * 4,
        out_specs=(pl.BlockSpec(memory_space=pltpu.VMEM), smem, smem),
        scratch_shapes=[
            pltpu.VMEM((rows, elec), BF16),
            pltpu.VMEM((elec, green_half.shape[2]), BF16),
            pltpu.VMEM((planes, walkers * elec, orb), BF16),
            pltpu.VMEM((planes, orb, rows), BF16),
            pltpu.VMEM((walkers, elec, rows), BF16),
            pltpu.VMEM((walkers, rows, elec), BF16),
            pltpu.VMEM((n, elec, rows), BF16),
            pltpu.VMEM((n - 1, elec, rows), BF16),
            pltpu.VMEM((n, rows, frame), BF16),
            pltpu.VMEM((spills, rows, LANES), BF16),
            pltpu.VMEM((8, rows), F32),
            pltpu.VMEM((n, 8, rows), BF16),
            pltpu.VMEM((walkers, 8, CHUNK), F32),
            pltpu.VMEM((walkers, rows, LANES), F32),
            pltpu.VMEM((n, 8, LANES), F32),
            dma((3,)),
            dma((2, n)),
            dma((2, planes, steps)),
            dma((planes, steps)),
            dma((bits_n, n)),
            dma((n,)),
            dma((bits_n, n, steps)),
            dma((n, steps)),
            dma((n, steps)),
            dma((n, steps)),
            dma((n,)),
            dma((n,)),
        ],
        compiler_params=pltpu.CompilerParams(
            collective_id=0, has_side_effects=True, vmem_limit_bytes=67043328
        ),
        name="energy",
    )(green_half, collocation, occupied.T, kernel)
    return potential, coulomb, exchange


def solution(mesh):
    placed = (P("wlk", None, None), P("wlk", "pts"), P("pts", None), P("pts", None))
    return jax.shard_map(
        local,
        mesh=mesh,
        in_specs=placed,
        out_specs=(P("wlk", "pts"), P("wlk"), P("wlk")),
        check_vma=False,
    )
```

time: 204 us -> 143 us (0.70)
  Pallas kernels: 197 us -> 139 us
  local copies, waits for them, and re-layouts: 5.95 us -> 3.62 us
    pallas_call x1, Pallas kernels: 197 us -> 139 us  [local(): pl.pallas_call(functools.partial(body, bits_n, planes, tuple(chunks), fra...]
    unnamed x4 -> x3, local copies, waits for them, and re-layouts: 5.95 us -> 3.62 us
where the time goes in v2:
time: 143 us
  Pallas kernels  139 us (97%)
  local copies, waits for them, and re-layouts  3.62 us (3%)
    pallas_call x1, Pallas kernels, local(): pl.pallas_call(functools.partial(body, bits_n, planes, tuple(chunks), fra...  139 us
    unnamed x3, local copies, waits for them, and re-layouts  3.62 us

profile of v2, /device:TPU:0, one launch (start us, length us, event | category | flops | bytes accessed | tf_op | source)
XLA Modules:
  0.0 143.1 jit_solution(15191524328788192290)
XLA Ops:
  0.6 138.8 %energy.1 = (f32[2,1200]{1,0:T(2,128)}, f32[2]{0:T(128)}, f32[2]{0:T(128)}) custom-call(bf16[2,400,2400]{2,1,0:T(8,128)(2,1)} %green_ref.1, bf16[600,1200]{1,0:T(8,128)(2,1)} %coll_ref.1, bf16[400,1200]{1,0:T(8,128)(2,1)} %bitcast.1, bf16[1200,9600]{1,0:T(8,128)(2,1)} %kern_ref.1), custom_call_target="tpu_custom_call" | custom-call | tf_op jit(solution)/shard_map/energy/pallas_call | solution.py:456
  139.5 1.3 copy.10
  140.8 1.1 copy.11
  141.9 1.2 copy.12

commit v3 on v2

--- a/solution.py
+++ b/solution.py
@@ -15,11 +15,11 @@
 
 
 def body(
-    bits_n, planes, chunks, frame, piece,
+    bits_n, planes, chunks, helped, frame, piece,
     green_ref, coll_ref, occ_ref, kern_ref,
-    pot_ref, coul_ref, exch_ref,
-    occ, gin, gs, xg, tht, thr, pht, thq, kal, kext, dens, dq, acc, pot, eall,
-    load_sem, kload_sem, zsend, zrecv, psend, precv, tsend, trecv, dsend, drecv, esend, erecv,
+    out_ref,
+    occ, gin, gs, gs2, tout, xg, tht, thr, pht, thq, kal, kext, dens, dq, acc, pot, eall,
+    load_sem, kload_sem, zsend, zrecv, psend, precv, tsend, trecv, dsend, drecv, esend, erecv, gsend, grecv, hsend, hrecv,
 ):
     n = 1 << bits_n
     rows, elec = occ.shape
@@ -46,8 +46,16 @@
     occ_load.start()
     x_load = pltpu.make_async_copy(coll_ref, xg.at[z], load_sem.at[1])
     x_load.start()
-    g_load = pltpu.make_async_copy(green_ref.at[0], gin, load_sem.at[2])
-    g_load.start()
+    slab = gin.shape[1]
+    slabs = [(w, r) for w in range(walkers) for r in range(0, elec, slab)]
+
+    def g_load(i):
+        w, r = slabs[i]
+        return pltpu.make_async_copy(green_ref.at[w, pl.ds(r, slab), :], gin.at[i % 2], load_sem.at[2 + i % 2])
+
+    g_load(0).start()
+    if len(slabs) > 1:
+        g_load(1).start()
 
     windows = []
     spill = 0
@@ -73,10 +81,6 @@
             )
         return copies
 
-    for b in range(n):
-        for copy in window(b):
-            copy.start()
-
     def realign(b):
         _, width, shift, extra = windows[b]
         for copy in window(b):
@@ -113,20 +117,30 @@
             src, xg.at[s, :, pl.ds(lo, wide)], zsend.at[way, s, k], zrecv.at[s, k], (me, there)
         )
 
+    first_helped = min(helped, default=steps)
+    at_end = (z == 0) | (z == planes - 1)
+    helping = (z == 1) | (z == planes - 2)
+
+    def low(k):
+        return 1 if k in helped else 0
+
     def z_own(k):
-        @pl.when(z > 0)
+        @pl.when(z > low(k))
         def _():
             z_copy(0, z, k, True).start()
 
-        @pl.when(z < planes - 1)
+        @pl.when(z < planes - 1 - low(k))
         def _():
             z_copy(1, z, k, True).start()
 
-    def ways(j):
-        return ((0, z + j < planes, z > 0, z + j), (1, z - j >= 0, z < planes - 1, z - j))
+    def ways(j, k):
+        return (
+            (0, z + j < planes, z > low(k), z + j),
+            (1, z - j >= 0, z < planes - 1 - low(k), z - j),
+        )
 
     def z_pass(k, j):
-        for way, ok, more, s in ways(j):
+        for way, ok, more, s in ways(j, k):
             @pl.when(ok & more)
             def _():
                 z_copy(way, s, k, False).wait_recv()
@@ -134,20 +148,81 @@
 
     def z_take(k):
         for j in range(1, planes):
-            for way, ok, more, s in ways(j):
-                @pl.when(ok & jnp.logical_not(more))
+            for way, ok, more, s in ways(j, k):
+                need = ok & jnp.logical_not(more)
+                if k in helped:
+                    need = need & jnp.logical_not(at_end | helping)
+
+                @pl.when(need)
                 def _():
                     z_copy(way, s, k, False).wait_recv()
 
     def z_done(k):
         for j in range(planes):
-            for way, ok, s in (
-                (0, (z + j < planes) & (z > 0), z + j),
-                (1, (z - j >= 0) & (z < planes - 1), z - j),
-            ):
-                @pl.when(ok)
+            for way, ok, more, s in ways(j, k):
+                @pl.when(ok & more)
                 def _():
                     z_copy(way, s, k, j == 0).wait_send()
+
+    end_to = z + 1 - 2 * (z // (planes - 1)) if planes > 1 else z
+    help_to = z - 1 + 2 * ((z + 1) // (planes - 1)) if planes > 1 else z
+    half = walkers * elec // 2
+
+    def g_part(ref, s, c):
+        return ref.at[s, pl.ds(pl.multiple_of(c * half, 16), half), :]
+
+    def g_out(s):
+        return remote(
+            g_part(gs, s, bit[0]), g_part(gs2, s, bit[0]), gsend.at[0, s], grecv.at[0, s], (me, end_to)
+        )
+
+    def g_share(s):
+        return remote(
+            g_part(gs2, s, bit[0]), g_part(gs2, s, bit[0]), gsend.at[1, s], grecv.at[1, s], (peer(1), z)
+        )
+
+    def g_got(s):
+        return remote(
+            g_part(gs2, s, 1 - bit[0]), g_part(gs2, s, 1 - bit[0]), gsend.at[1, s], grecv.at[1, s], (peer(1), z)
+        )
+
+    def g_first():
+        if helped:
+            @pl.when(helping)
+            def _():
+                for s in range(planes):
+                    g_out(s).wait_recv()
+                    g_share(s).start()
+
+    def h_copy(k):
+        lo, wide = chunks[k]
+        base = chunks[first_helped][0]
+        return remote(
+            tout.at[:, :, pl.ds(lo - base, wide)], tht.at[:, :, pl.ds(lo, wide)],
+            hsend.at[k - first_helped], hrecv.at[k - first_helped], (me, help_to),
+        )
+
+    def help_end(k):
+        if k in helped:
+            lo, wide = chunks[k]
+            base = chunks[first_helped][0]
+
+            @pl.when(helping)
+            def _():
+                for s in range(planes):
+                    g_got(s).wait_recv()
+                for j in range(1, planes):
+                    for way, ok, more, s in ways(j, k):
+                        @pl.when(ok & jnp.logical_not(more))
+                        def _():
+                            z_copy(way, s, k, False).wait_recv()
+                total = None
+                for s in range(planes):
+                    part = jnp.dot(gs2[s], xg[s, :, pl.ds(lo, wide)], preferred_element_type=F32)
+                    total = part if total is None else total + part
+                for w in range(walkers):
+                    tout[w, :, pl.ds(lo - base, wide)] = total[w * elec : (w + 1) * elec].astype(BF16)
+                h_copy(k).start()
 
     def occ_copy(t, d):
         return remote(
@@ -175,6 +250,15 @@
     z_own(0)
     if steps > 1:
         z_own(1)
+    if helped:
+        @pl.when(at_end)
+        def _():
+            for k in range(2, steps):
+                z_own(k)
+
+    for b in range(n):
+        for copy in window(b):
+            copy.start()
 
     acc[...] = jnp.zeros_like(acc)
     pot[...] = jnp.zeros_like(pot)
@@ -202,13 +286,17 @@
                 if e in ds:
                     occ_copy(later, e).start()
 
-    for w in range(walkers):
-        g_load.wait()
+    for i, (w, r) in enumerate(slabs):
+        g_load(i).wait()
         for s in range(planes):
-            gs[s, pl.ds(w * elec, elec), :] = gin[:, s * orb : (s + 1) * orb]
-        if w + 1 < walkers:
-            g_load = pltpu.make_async_copy(green_ref.at[w + 1], gin, load_sem.at[2])
-            g_load.start()
+            gs[s, pl.ds(w * elec + r, slab), :] = gin[i % 2, :, s * orb : (s + 1) * orb]
+        if i + 2 < len(slabs):
+            g_load(i + 2).start()
+    if helped:
+        @pl.when(at_end)
+        def _():
+            for s in range(planes):
+                g_out(s).start()
 
     th_plan = []
     held = [0]
@@ -218,13 +306,26 @@
 
     def theta(k):
         lo, valid = chunks[k]
-        total = None
-        for s in range(planes):
-            part = jnp.dot(gs[s], xg[s, :, pl.ds(lo, valid)], preferred_element_type=F32)
-            total = part if total is None else total + part
-        for w in range(walkers):
-            one = total[w * elec : (w + 1) * elec].astype(BF16)
-            tht[w, :, pl.ds(lo, valid)] = one
+
+        def make():
+            total = None
+            for s in range(planes):
+                part = jnp.dot(gs[s], xg[s, :, pl.ds(lo, valid)], preferred_element_type=F32)
+                total = part if total is None else total + part
+            for w in range(walkers):
+                tht[w, :, pl.ds(lo, valid)] = total[w * elec : (w + 1) * elec].astype(BF16)
+
+        if k in helped:
+            pl.when(jnp.logical_not(at_end))(make)
+
+            @pl.when(at_end)
+            def _():
+                remote(
+                    tht.at[:, :, pl.ds(lo, valid)], tht.at[:, :, pl.ds(lo, valid)],
+                    hsend.at[k - first_helped], hrecv.at[k - first_helped], (me, end_to),
+                ).wait_recv()
+        else:
+            make()
         for w in range(walkers):
             turned = tht[w, :, pl.ds(lo, valid)]
             thr[w, pl.ds(lo, valid), :] = turned.T
@@ -317,7 +418,9 @@
                 fold(w, me, 0, rhs, 0, lo, lo, wide, 2.0)
             fold(w, me, 0, rhs, lo, wide, lo, wide, 1.0)
 
-        spread(0, kal[me, :, pl.ds(lo, wide)].astype(F32), 0, rows, lo, wide)
+        for p0 in range(0, rows, 2 * CHUNK):
+            pm = min(2 * CHUNK, rows - p0)
+            spread(0, kal[me, pl.ds(p0, pm), pl.ds(lo, wide)].astype(F32), p0, pm, lo, wide)
 
     def exchange_new(k, services):
         lo, wide = chunks[k]
@@ -336,8 +439,10 @@
                         serve()
 
             b, w = pair(d)
-            kf = fold(w, b, d, thq[d - 1, :, pl.ds(lo, wide)], 0, full, lo, wide, 2.0)
-            spread(d, kf, 0, full, lo, wide)
+            for p0 in range(0, full, 2 * CHUNK):
+                pm = min(2 * CHUNK, full - p0)
+                kf = fold(w, b, d, thq[d - 1, :, pl.ds(lo, wide)], p0, pm, lo, wide, 2.0)
+                spread(d, kf, p0, pm, lo, wide)
 
     def near_pass(k):
         if k < steps:
@@ -350,7 +455,10 @@
 
     def own_send(k):
         if 1 < k < steps:
-            z_own(k)
+            if helped:
+                pl.when(jnp.logical_not(at_end))(lambda: z_own(k))
+            else:
+                z_own(k)
 
     def first_arrivals(k):
         for i, (t, d) in enumerate(arrivals):
@@ -392,6 +500,13 @@
             exchange_all(0, {n - 2: [functools.partial(first_arrivals, 1)]})
         if k == steps - 1:
             exchange_new(k - 1, {n - 3: [functools.partial(first_arrivals, k)]})
+        elif k == steps - 3 and helped:
+            exchange_old(k)
+            exchange_own(k)
+            first_arrivals(k)
+            g_first()
+            help_end(steps - 1)
+            exchange_new(k, {})
         elif k < steps - 2:
             exchange_all(k, {})
     exchange_old(steps - 1)
@@ -401,7 +516,7 @@
     pot_rows = []
     for w in range(walkers):
         pot_rows.append(jnp.sum(pot[w].T, axis=0, keepdims=True))
-        pot_ref[pl.ds(w, 1), :] = pot_rows[w]
+        out_ref[pl.ds(w, 1), pl.ds(0, rows)] = pot_rows[w]
     for w in range(walkers):
         eall[me, pl.ds(w, 1), :] = jnp.full((1, LANES), 0.5 * jnp.sum(dens[pl.ds(w, 1), :] * pot_rows[w]), F32)
         eall[me, pl.ds(walkers + w, 1), :] = jnp.full((1, LANES), -0.5 * jnp.sum(acc[w]), F32)
@@ -419,15 +534,26 @@
     whole = eall[0]
     for b in range(1, n):
         whole = whole + eall[b]
-    for w in range(walkers):
-        coul_ref[w] = whole[w, 0]
-        exch_ref[w] = whole[walkers + w, 0]
+    out_ref[:, pl.ds(frame, LANES)] = whole[: 2 * walkers]
 
     for d in range(1, n):
         e_copy(d).wait_send()
     for t, deltas in plan:
         for d in deltas:
             occ_copy(t, d).wait_send()
+    if helped:
+        @pl.when(at_end)
+        def _():
+            for s in range(planes):
+                g_out(s).wait_send()
+
+        @pl.when(helping)
+        def _():
+            for s in range(planes):
+                g_share(s).wait_send()
+            for k in helped:
+                h_copy(k).wait_send()
+
     for k in range(steps):
         z_done(k)
         for t, deltas in th_plan:
@@ -448,24 +574,24 @@
     for lo in range(0, rows, CHUNK):
         chunks.append((lo, min(CHUNK, rows - lo)))
     steps = len(chunks)
+    helped = (steps - 1,) if planes >= 4 and steps >= 4 and walkers * elec % 32 == 0 else ()
+    late = chunks[helped[0]][0] if helped else 0
+    slab = max([r for r in range(16, 96, 16) if elec % r == 0] or [elec])
     spills = max(1, sum((rows * b) % LANES + rows > frame for b in range(n)))
     piece = max([r for r in range(16, 256, 16) if rows % r == 0] or [rows])
     anywhere = pl.BlockSpec(memory_space=pl.ANY)
-    smem = pl.BlockSpec(memory_space=pltpu.SMEM)
     dma = pltpu.SemaphoreType.DMA
-    potential, coulomb, exchange = pl.pallas_call(
-        functools.partial(body, bits_n, planes, tuple(chunks), frame, piece),
-        out_shape=(
-            jax.ShapeDtypeStruct((walkers, rows), F32),
-            jax.ShapeDtypeStruct((walkers,), F32),
-            jax.ShapeDtypeStruct((walkers,), F32),
-        ),
+    out = pl.pallas_call(
+        functools.partial(body, bits_n, planes, tuple(chunks), helped, frame, piece),
+        out_shape=jax.ShapeDtypeStruct((2 * walkers, frame + LANES), F32),
         in_specs=[anywhere] * 4,
-        out_specs=(pl.BlockSpec(memory_space=pltpu.VMEM), smem, smem),
+        out_specs=pl.BlockSpec(memory_space=pltpu.VMEM),
         scratch_shapes=[
             pltpu.VMEM((rows, elec), BF16),
-            pltpu.VMEM((elec, green_half.shape[2]), BF16),
+            pltpu.VMEM((2, slab, green_half.shape[2]), BF16),
             pltpu.VMEM((planes, walkers * elec, orb), BF16),
+            pltpu.VMEM((planes, walkers * elec, orb) if helped else (1, 16, LANES), BF16),
+            pltpu.VMEM((walkers, elec, rows - late) if helped else (1, 16, LANES), BF16),
             pltpu.VMEM((planes, orb, rows), BF16),
             pltpu.VMEM((walkers, elec, rows), BF16),
             pltpu.VMEM((walkers, rows, elec), BF16),
@@ -478,7 +604,7 @@
             pltpu.VMEM((walkers, 8, CHUNK), F32),
             pltpu.VMEM((walkers, rows, LANES), F32),
             pltpu.VMEM((n, 8, LANES), F32),
-            dma((3,)),
+            dma((4,)),
             dma((2, n)),
             dma((2, planes, steps)),
             dma((planes, steps)),
@@ -490,13 +616,17 @@
             dma((n, steps)),
             dma((n,)),
             dma((n,)),
+            dma((2, planes)),
+            dma((2, planes)),
+            dma((steps,)),
+            dma((steps,)),
         ],
         compiler_params=pltpu.CompilerParams(
             collective_id=0, has_side_effects=True, vmem_limit_bytes=67043328
         ),
         name="energy",
     )(green_half, collocation, occupied.T, kernel)
-    return potential, coulomb, exchange
+    return out[:walkers, :rows], out[:walkers, frame], out[walkers:, frame]
 
 
 def solution(mesh):

time: 143 us -> 139 us (0.972); the launches traced: 143 us -> 137 us
  Pallas kernels: 139 us -> 134 us
    pallas_call x1, Pallas kernels: 139 us -> 134 us  [local(): pl.pallas_call(functools.partial(body, bits_n, planes, tuple(chunks), hel...]
    unnamed x3 -> x0, local copies, waits for them, and re-layouts: 3.62 us -> none
    slice x0 -> x2, local copies, waits for them, and re-layouts: none -> 2.74 us  [local(): return (out[:walkers, :rows], out[:walkers, frame], out[walkers:, frame])]
where the time goes in v3:
time: 139 us; the launch traced here: 137 us
  Pallas kernels  134 us (96%)
  local copies, waits for them, and re-layouts  2.74 us (2%)
    pallas_call x1, Pallas kernels, local(): pl.pallas_call(functools.partial(body, bits_n, planes, tuple(chunks), hel...  134 us

profile of v3, /device:TPU:0, one launch (start us, length us, event | category | flops | bytes accessed | tf_op | source)
XLA Modules:
  0.0 136.9 jit_solution(11961245917672942127)
XLA Ops:
  0.6 133.5 %energy.1 = f32[4,1408]{1,0:T(4,128)} custom-call(bf16[2,400,2400]{2,1,0:T(8,128)(2,1)} %green_ref.1, bf16[600,1200]{1,0:T(8,128)(2,1)} %coll_ref.1, bf16[400,1200]{1,0:T(8,128)(2,1)} %bitcast.1, bf16[1200,9600]{1,0:T(8,128)(2,1)} %kern_ref.1), custom_call_target="tpu_custom_call" | custom-call | tf_op jit(solution)/shard_map/energy/pallas_call | solution.py:584
  134.2 1.4 %slice_reduce_fusion = (f32[2]{0:T(128)}, f32[2]{0:T(128)}) fusion(f32[4,1408]{1,0:T(4,128)} %energy.1), kind=kLoop, calls=%fused_computation | loop fusion | bytes 32 | tf_op jit(solution)/shard_map/slice | solution.py:629
  135.6 1.3 slice.9

commit v4 on v3

--- a/solution.py
+++ b/solution.py
@@ -256,17 +256,10 @@
             for k in range(2, steps):
                 z_own(k)
 
-    for b in range(n):
-        for copy in window(b):
-            copy.start()
-
+    occ_load.wait()
     acc[...] = jnp.zeros_like(acc)
     pot[...] = jnp.zeros_like(pot)
     dens[...] = jnp.zeros_like(dens)
-    occ_load.wait()
-    for lo, wide in chunks:
-        occ[pl.ds(lo, wide), :] = pht[0, :, pl.ds(lo, wide)].T
-
     chip_bits = list(range(1, bits_n))
     held = [0]
     sent = []
@@ -276,6 +269,11 @@
         held = held + [d ^ (1 << t) for d in held]
     for t, _ in plan:
         occ_copy(t, 0).start()
+    for b in range(n):
+        for copy in window(b):
+            copy.start()
+    for lo, wide in chunks:
+        occ[pl.ds(lo, wide), :] = pht[0, :, pl.ds(lo, wide)].T
 
     def occ_pass(step):
         t, deltas = plan[step]
@@ -327,15 +325,16 @@
         else:
             make()
         for w in range(walkers):
+            thr[w, pl.ds(lo, valid), :] = tht[w, :, pl.ds(lo, valid)].T
+        for t, _ in th_plan:
+            th_copy(t, 0, k).start()
+        for w in range(walkers):
             turned = tht[w, :, pl.ds(lo, valid)]
-            thr[w, pl.ds(lo, valid), :] = turned.T
             value = jnp.sum(
                 turned.astype(F32) * pht[0, :, pl.ds(lo, valid)].astype(F32), axis=0, keepdims=True
             )
             dens[pl.ds(w, 1), pl.ds(lo, valid)] = value
         dq[0, :, pl.ds(lo, valid)] = dens[:, pl.ds(lo, valid)].astype(BF16)
-        for t, _ in th_plan:
-            th_copy(t, 0, k).start()
         for d in range(1, n):
             d_copy(d, k).start()
 
@@ -397,16 +396,17 @@
             w = w + jnp.where(d // (1 << t) == 1, bit[t], 0)
         return b, w
 
-    def exchange_old(k):
+    def exchange_old(k, upto=None):
         lo, wide = chunks[k]
-        if k == 0:
+        upto = lo if upto is None else upto
+        if upto == 0:
             return
 
         @pl.loop(1, n)
         def _(d):
             b, w = pair(d)
-            kf = fold(w, b, d, thq[d - 1, :, pl.ds(0, lo)], lo, wide, 0, lo, 2.0)
-            spread(d, kf, lo, wide, 0, lo)
+            kf = fold(w, b, d, thq[d - 1, :, pl.ds(0, upto)], lo, wide, 0, upto, 2.0)
+            spread(d, kf, lo, wide, 0, upto)
 
     def exchange_own(k):
         lo, wide = chunks[k]
@@ -422,9 +422,9 @@
             pm = min(2 * CHUNK, rows - p0)
             spread(0, kal[me, pl.ds(p0, pm), pl.ds(lo, wide)].astype(F32), p0, pm, lo, wide)
 
-    def exchange_new(k, services):
+    def exchange_new(k, services, full=None):
         lo, wide = chunks[k]
-        full = lo + wide
+        full = lo + wide if full is None else full
 
         @pl.loop(0, n - 1)
         def _(i):
@@ -499,7 +499,9 @@
         if k == 1 and k < steps - 1:
             exchange_all(0, {n - 2: [functools.partial(first_arrivals, 1)]})
         if k == steps - 1:
-            exchange_new(k - 1, {n - 3: [functools.partial(first_arrivals, k)]})
+            exchange_old(k, chunks[k - 1][0])
+            exchange_own(k)
+            exchange_new(k - 1, {n // 2: [functools.partial(first_arrivals, k)]}, rows)
         elif k == steps - 3 and helped:
             exchange_old(k)
             exchange_own(k)
@@ -509,8 +511,8 @@
             exchange_new(k, {})
         elif k < steps - 2:
             exchange_all(k, {})
-    exchange_old(steps - 1)
-    exchange_own(steps - 1)
+    if steps == 1:
+        exchange_own(0)
     exchange_new(steps - 1, {})
 
     pot_rows = []

time: 139 us -> 134 us (0.964)
  Pallas kernels: 134 us -> 129 us
    pallas_call x1, Pallas kernels: 134 us -> 129 us  [local(): pl.pallas_call(functools.partial(body, bits_n, planes, tuple(chunks), hel...]
where the time goes in v4:
time: 134 us; the launch traced here: 133 us
  Pallas kernels  129 us (96%)
  local copies, waits for them, and re-layouts  2.74 us (2%)
    pallas_call x1, Pallas kernels, local(): pl.pallas_call(functools.partial(body, bits_n, planes, tuple(chunks), hel...  129 us
    slice x2, local copies, waits for them, and re-layouts, local(): return (out[:walkers, :rows], out[:walkers, frame], out[walkers:, frame])  2.74 us

profile of v4, /device:TPU:0, one launch (start us, length us, event | category | flops | bytes accessed | tf_op | source)
XLA Modules:
  0.0 132.6 jit_solution(1816379071871917242)
XLA Ops:
  0.6 129.2 %energy.1 = f32[4,1408]{1,0:T(4,128)} custom-call(bf16[2,400,2400]{2,1,0:T(8,128)(2,1)} %green_ref.1, bf16[600,1200]{1,0:T(8,128)(2,1)} %coll_ref.1, bf16[400,1200]{1,0:T(8,128)(2,1)} %bitcast.1, bf16[1200,9600]{1,0:T(8,128)(2,1)} %kern_ref.1), custom_call_target="tpu_custom_call" | custom-call | tf_op jit(solution)/shard_map/energy/pallas_call | solution.py:586
  129.8 1.4 %slice_reduce_fusion = (f32[2]{0:T(128)}, f32[2]{0:T(128)}) fusion(f32[4,1408]{1,0:T(4,128)} %energy.1), kind=kLoop, calls=%fused_computation | loop fusion | bytes 32 | tf_op jit(solution)/shard_map/slice | solution.py:631
  131.2 1.3 %slice.9 = f32[2,1200]{1,0:T(2,128)} slice(f32[4,1408]{1,0:T(4,128)} %energy.1), slice={[0:2], [0:1200]} | slice | bytes 19200 | tf_op jit(solution)/shard_map/slice | solution.py:631
